TPU v7x, 32 devices: a whole 2x2x4 slice. The times are simulated.
32 devices in a mesh: scen: 2 (over x), lon: 16 (over z, y, core).
Axes of the slice: x: 2, y: 2, z: 4, core: 2. Of those that a mesh axis runs over, the one named last changes fastest.
Arguments:
- tracer: float32 [16, 4, 512, 1024], P('scen', None, 'lon'), parts along dimension 0, may hold values from 0.25 to 15, as said below
- offsets: int32 [4, 512, 1024], P(None, 'lon'), may hold values from -12 to 12
- frac: float32 [4, 1024], replicated, may hold values from 0.02 to 0.98
- air_before: float32 [4, 512, 1024], P(None, 'lon'), may hold values from 0.5 to 2
- air_after: float32 [4, 512, 1024], P(None, 'lon'), may hold values from 0.05 to 15, as said below
- growth: float32 [16], P('scen'), parts along dimension 0, may hold values from 0.05 to 0.5
Outputs:
- tracer_next: float32 [16, 4, 512, 1024], P('scen', None, 'lon'), parts along dimension 0
There are 2 independent parts, one for each index of `scen`. A program takes and returns all parts, laid end to end along the dimension named above; an argument that names none is the same for every part. Nothing has to cross between parts.
Inputs may be any that keep to these rules, and one draw needn't show every extreme that they name: `tracer`: positive mixing ratios. `air_after`: positive air masses.
All inputs are finite; a program needn't handle non-finite values.
Results may differ from a plain program's by a relative error of at most 0.00002.
Values sent between devices are 32-bit elements; how exact they have to be, the bound alone decides.
A program may use at most 64 MiB of HBM per device.

v0:
```python
import jax
import jax.numpy as jnp
from jax import lax
from jax.sharding import PartitionSpec as P

OFFMAX = 12


def with_halo(block, sides, width):
    for axis, dim in sides:
        count = lax.axis_size(axis)
        forward = [(i, i + 1) for i in range(count - 1)]
        forward.append((count - 1, 0))
        backward = [(target, source) for source, target in forward]
        low = lax.ppermute(
            lax.slice_in_dim(block, block.shape[dim] - width, None, axis=dim), axis, forward
        )
        high = lax.ppermute(lax.slice_in_dim(block, 0, width, axis=dim), axis, backward)
        block = jnp.concatenate([low, block, high], axis=dim)
    return block


def cubic_weights(fraction):
    first = -fraction * (1.0 - fraction) * (2.0 - fraction) / 6.0
    second = (1.0 + fraction) * (1.0 - fraction) * (2.0 - fraction) / 2.0
    third = (1.0 + fraction) * fraction * (2.0 - fraction) / 2.0
    fourth = -(1.0 + fraction) * fraction * (1.0 - fraction) / 6.0
    return (first, second, third, fourth)


def limited_values(padded, offsets, weights, margin, furthest):
    span_cols = offsets.shape[1]
    lon_dim = padded.ndim - 2
    empty = jnp.zeros(padded.shape[:-2] + (span_cols, padded.shape[-1]), jnp.float32)
    stencil = [empty, empty, empty, empty]
    for offset_value in range(-furthest, furthest + 1):
        chosen = offsets == offset_value
        for offset_tap in range(4):
            begin_at = margin - offset_value - 1 + offset_tap
            window = lax.slice_in_dim(padded, begin_at, begin_at + span_cols, axis=lon_dim)
            stencil[offset_tap] = jnp.where(chosen, window, stencil[offset_tap])
    cubic = weights[0] * stencil[0] + weights[1] * stencil[1]
    cubic = cubic + weights[2] * stencil[2] + weights[3] * stencil[3]
    lower_bound = jnp.minimum(stencil[1], stencil[2])
    upper_bound = jnp.maximum(stencil[1], stencil[2])
    return jnp.clip(cubic, lower_bound, upper_bound)


def on_device(tracer, offsets, frac, air_before, air_after, growth):
    margin = OFFMAX + 2
    weights = tuple((item[:, None, :] for item in cubic_weights(frac)))
    before_local = jnp.sum(tracer * air_before[None], axis=(1, 2, 3))
    before_total = lax.psum(before_local, "lon")
    padded = with_halo(tracer, (("lon", 2),), margin)
    limited = limited_values(padded, offsets, weights, margin, OFFMAX)
    after_local = jnp.sum(limited * air_after[None], axis=(1, 2, 3))
    after_total = lax.psum(after_local, "lon")
    factor = before_total * (1.0 + growth) / after_total
    return limited * factor[:, None, None, None]


def solution(mesh):
    placed = (
        P("scen", None, "lon", None),
        P(None, "lon", None),
        P(),
        P(None, "lon", None),
        P(None, "lon", None),
        P("scen"),
    )
    return jax.shard_map(
        on_device,
        mesh=mesh,
        in_specs=placed,
        out_specs=P("scen", None, "lon", None),
        check_vma=False,
    )
```

profile of v0, /device:TPU:0, one launch (start us, length us, event | category | flops | bytes accessed | tf_op | source)
XLA Modules:
  0.0 135.8 jit_solution(8075920262998058468)
XLA Ops:
  0.0 3.0 %fusion.51 = (f32[8,4,14,1024]{3,2,1,0:T(8,128)S(1)}, f32[8,4,14,1024]{3,2,1,0:T(8,128)S(1)}) fusion(f32[8,4,32,1024]{3,2,1,0:T(8,128)} %param.6), kind=kLoop, calls=%fused_computation.111 | loop fusion | bytes 7340032 | tf_op jit(solution)/shard_map/slice | solution.py:16
  3.0 0.0 copy-start.4
  3.0 0.0 copy-start
  3.0 0.0 copy-start.2
  3.0 1.1 copy.11
  4.1 0.5 collective-permute-start
  4.6 1.1 copy.12
  5.7 5.2 %collective-permute-start.1 = (f32[8,4,14,1024]{3,0,2,1:T(8,128)S(1)}, f32[8,4,14,1024]{3,0,2,1:T(8,128)S(1)}, u32[]{:S(2)}, u32[]{:S(2)}) collective-permute-start(f32[8,4,14,1024]{3,0,2,1:T(8,128)S(1)} %copy.12), channel_id=1, source_target_pairs={{1,0},{2,1},{3,2},{4,3},{5,4},{6,5},{7,6},{8,7},{9,8},{10,9},{11,1... | collective-permute-start | bytes 5505032 | tf_op jit(solution)/shard_map/ppermute | solution.py:18
  10.9 0.0 copy-done.4
  11.0 0.0 copy-done
  11.0 0.0 copy-done.2
  11.0 0.0 copy-start.3
  11.0 1.6 %multiply_reduce_fusion.1 = (f32[8]{0:T(128)}, f32[8,4,46,1024]{3,2,1,0:T(8,128)S(1)}) fusion(f32[8,4,32,1024]{3,2,1,0:T(8,128)S(1)} %copy-done, f32[4,32,1024]{2,1,0:T(8,128)S(1)} %copy-done.2), kind=kLoop, calls=%fused_computation.70 | loop fusion | flops 2097143 | bytes 8912928 | tf_op jit(solution)/shard_map/reduce_sum | solution.py:52
  12.6 0.0 copy-done.3
  12.6 2.7 %broadcast_compare_fusion.24 = (pred[4,32,1024]{2,1,0:T(8,128)(4,1)S(1)}, pred[4,32,1024]{2,1,0:T(8,128)(4,1)S(1)}, pred[4,32,1024]{2,1,0:T(8,128)(4,1)S(1)}, pr...) fusion(s32[4,32,1024]{2,1,0:T(8,128)S(1)} %copy-done.3), kind=kLoop, calls=%fused_computation.97 | loop fusion | flops 3276800 | bytes 3801088 | tf_op jit(solution)/shard_map/eq | solution.py:37
  15.3 0.0 copy-start.1
  15.3 15.3 %collective-permute-done = f32[8,4,14,1024]{3,0,2,1:T(8,128)S(1)} collective-permute-done((f32[8,4,14,1024]{3,0,2,1:T(8,128)S(1)}, f32[8,4,14,1024]{3,0,2,1:T(8,128)S(1)}, u32[]{:S(2)}, u32[]{:S(2)}) %collective-permute-start) | collective-permute-done | bytes 1835040 | tf_op jit(solution)/shard_map/ppermute | solution.py:15
  30.6 1.1 copy.8
  31.7 0.0 collective-permute-done.1
  31.7 1.1 copy_dynamic-update-slice_fusion
  32.8 0.0 copy-done.1
  32.8 49.5 %multiply_reduce_fusion = (f32[8]{0:T(128)S(1)}, f32[8,4,32,1024]{3,2,1,0:T(8,128)}) fusion(f32[4,32,1024]{2,1,0:T(8,128)S(1)} %copy-done.1, f32[8,4,32,1024]{3,2,1,0:T(8,128)} %param.6, f32[8,4,46,1024]{3,2,1,0:T(8,128)S(1)} %copy_dynamic-update-slice_fusion, f32[4,1024]{1,0:T(4,128)S(1)} %get-tuple-element.40, f32[4,1024]{1,0:T(4,128)S(1)} %get-tuple-element.41, ...), kind=kLoop, calls=%fused_computation.69 | loop fusion | flops 132120568 | bytes 72810528 | tf_op jit(solution)/shard_map/reduce_sum | solution.py:56
  82.3 47.8 %all-reduce = (f32[8]{0:T(128)S(1)}, f32[8]{0:T(128)S(1)}) all-reduce(f32[8]{0:T(128)S(1)} %get-tuple-element.7, f32[8]{0:T(128)} %get-tuple-element.9), channel_id=1, replica_groups=mesh['scen'=2,'lon'=16] {'lon'}, use_global_device_ids=true, to_apply=%region_3.4 | all-reduce | flops 16 | bytes 128 | tf_op jit(solution)/shard_map/psum | solution.py:57
  130.1 0.7 multiply_divide_fusion
  130.7 5.1 %broadcast_multiply_fusion = f32[8,4,32,1024]{3,2,1,0:T(8,128)} fusion(f32[8,4,32,1024]{3,2,1,0:T(8,128)} %get-tuple-element.8, f32[8]{0:T(128)S(1)} %multiply_divide_fusion), kind=kLoop, calls=%fused_computation.72 | loop fusion | flops 1048576 | bytes 8388640 | tf_op jit(solution)/shard_map/mul | solution.py:59
  (1 shorter events, 0.0 us)
Async XLA Ops:
  3.0 8.0 %copy-start.4 = (f32[4,1024]{1,0:T(4,128)S(1)}, f32[4,1024]{1,0:T(4,128)}, u32[]{:S(2)}) copy-start(f32[4,1024]{1,0:T(4,128)} %param.8) | copy-start | bytes 49156
  3.0 8.0 %copy-start = (f32[8,4,32,1024]{3,2,1,0:T(8,128)S(1)}, f32[8,4,32,1024]{3,2,1,0:T(8,128)}, u32[]{:S(2)}) copy-start(f32[8,4,32,1024]{3,2,1,0:T(8,128)} %param.6) | copy-start | bytes 12582916
  3.0 8.0 %copy-start.2 = (f32[4,32,1024]{2,1,0:T(8,128)S(1)}, f32[4,32,1024]{2,1,0:T(8,128)}, u32[]{:S(2)}) copy-start(f32[4,32,1024]{2,1,0:T(8,128)} %param.9) | copy-start | bytes 1572868
  4.1 26.5 %collective-permute-start = (f32[8,4,14,1024]{3,0,2,1:T(8,128)S(1)}, f32[8,4,14,1024]{3,0,2,1:T(8,128)S(1)}, u32[]{:S(2)}, u32[]{:S(2)}) collective-permute-start(f32[8,4,14,1024]{3,0,2,1:T(8,128)S(1)} %copy.11), channel_id=1, source_target_pairs={{0,1},{1,2},{2,3},{3,4},{4,5},{5,6},{6,7},{7,8},{8,9},{9,10},{10,1... | collective-permute-start | bytes 5505032 | tf_op jit(solution)/shard_map/ppermute | solution.py:15
  5.7 26.0 %collective-permute-start.1 = (f32[8,4,14,1024]{3,0,2,1:T(8,128)S(1)}, f32[8,4,14,1024]{3,0,2,1:T(8,128)S(1)}, u32[]{:S(2)}, u32[]{:S(2)}) collective-permute-start(f32[8,4,14,1024]{3,0,2,1:T(8,128)S(1)} %copy.12), channel_id=1, source_target_pairs={{1,0},{2,1},{3,2},{4,3},{5,4},{6,5},{7,6},{8,7},{9,8},{10,9},{11,1... | collective-permute-start | bytes 5505032 | tf_op jit(solution)/shard_map/ppermute | solution.py:18
  11.0 1.6 %copy-start.3 = (s32[4,32,1024]{2,1,0:T(8,128)S(1)}, s32[4,32,1024]{2,1,0:T(8,128)}, u32[]{:S(2)}) copy-start(s32[4,32,1024]{2,1,0:T(8,128)} %param.7) | copy-start | bytes 1572868
  15.3 17.5 %copy-start.1 = (f32[4,32,1024]{2,1,0:T(8,128)S(1)}, f32[4,32,1024]{2,1,0:T(8,128)}, u32[]{:S(2)}) copy-start(f32[4,32,1024]{2,1,0:T(8,128)} %param.10) | copy-start | bytes 1572868
where the time goes:
time: 136 us
  other arithmetic  59.5 us (44%)
  blocking collectives  47.8 us (35%)
  waiting for transfers between devices  15.3 us (11%)
  local copies, waits for them, and re-layouts  7.3 us (5%)
  starting transfers between devices  5.78 us (4%)
    reduce_sum x1, other arithmetic, on_device(): after_local = jnp.sum(limited * air_after[None], axis=(1, 2, 3))  49.5 us
    psum x1, blocking collectives, on_device(): after_total = lax.psum(after_local, 'lon')  47.8 us
    ppermute x1, waiting for transfers between devices, with_halo(): lax.ppermute(lax.slice_in_dim(block, block.shape[dim] - width, None, axis...  15.3 us
    ppermute x1, starting transfers between devices, with_halo(): lax.ppermute(lax.slice_in_dim(block, 0, width, axis=dim), axis, backward)  5.23 us
    mul x1, other arithmetic, on_device(): return limited * factor[:, None, None, None]  5.11 us
    slice x1, local copies, waits for them, and re-layouts, with_halo(): lax.slice_in_dim(block, block.shape[dim] - width, None, axis=dim)  2.98 us
  transfers between devices with their start and end apart: 2, of which 1 were waited for; matrix products, arithmetic and copies ran while one was open for 5% of the time, Pallas kernels for 0%

commit v1 on v0

v1 whole, which is shorter than its diff:
```python
import functools

import jax
import jax.numpy as jnp
from jax import lax
from jax.experimental import pallas as pl
from jax.experimental.pallas import tpu as pltpu
from jax.sharding import PartitionSpec as P

OFFMAX = 12
LOW = OFFMAX + 1
HIGH = OFFMAX + 2
LANES = 128
SUB = 8
SPLITS = 2
MESH = pl.DeviceIdType.MESH


def cubic_weights(fraction):
    first = -fraction * (1.0 - fraction) * (2.0 - fraction) / 6.0
    second = (1.0 + fraction) * (1.0 - fraction) * (2.0 - fraction) / 2.0
    third = (1.0 + fraction) * fraction * (2.0 - fraction) / 2.0
    fourth = -(1.0 + fraction) * fraction * (1.0 - fraction) / 6.0
    return (first, second, third, fourth)


def transport_kernel(
    count,
    growth_ref,
    tracer_hbm,
    offsets_hbm,
    frac_ref,
    before_hbm,
    after_hbm,
    limited_hbm,
    factor_ref,
    tracer,
    limited,
    offsets,
    air_before,
    air_after,
    send_low,
    send_high,
    recv_low,
    recv_high,
    padded,
    sums,
    mine,
    masses,
    load_sem,
    air_sem,
    store_sem,
    send_sem,
    recv_sem,
    mass_send,
    mass_recv,
):
    species, levels, rows, lats = tracer.shape
    chunks = levels * SPLITS
    blocks = lats // LANES // SPLITS
    width = blocks * LANES
    me = lax.axis_index("lon")
    right = lax.rem(me + 1, count)
    left = lax.rem(me + count - 1, count)
    span = rows + 2 * OFFMAX

    def load(chunk):
        level = chunk // SPLITS
        lanes = pl.ds(pl.multiple_of(lax.rem(chunk, SPLITS) * width, width), width)
        return pltpu.make_async_copy(
            tracer_hbm.at[:, level, :, lanes], tracer.at[:, level, :, lanes], load_sem.at[chunk]
        )

    def store(chunk):
        level = chunk // SPLITS
        lanes = pl.ds(pl.multiple_of(lax.rem(chunk, SPLITS) * width, width), width)
        return pltpu.make_async_copy(
            limited.at[:, level, :, lanes], limited_hbm.at[:, level, :, lanes], store_sem.at[chunk]
        )

    airs = [
        pltpu.make_async_copy(before_hbm, air_before, air_sem.at[0]),
        pltpu.make_async_copy(offsets_hbm, offsets, air_sem.at[1]),
        pltpu.make_async_copy(after_hbm, air_after, air_sem.at[2]),
    ]

    def forward(chunk):
        return pltpu.make_async_remote_copy(
            src_ref=send_low.at[chunk],
            dst_ref=recv_low.at[chunk],
            send_sem=send_sem.at[0, chunk],
            recv_sem=recv_sem.at[0, chunk],
            device_id={"lon": right},
            device_id_type=MESH,
        )

    def backward(chunk):
        return pltpu.make_async_remote_copy(
            src_ref=send_high.at[chunk],
            dst_ref=recv_high.at[chunk],
            send_sem=send_sem.at[1, chunk],
            recv_sem=recv_sem.at[1, chunk],
            device_id={"lon": left},
            device_id_type=MESH,
        )

    barrier = pltpu.get_barrier_semaphore()

    @pl.loop(1, count)
    def _(step):
        peer = lax.rem(me + step, count)
        pl.semaphore_signal(barrier, inc=1, device_id={"lon": peer}, device_id_type=MESH)

    @pl.loop(0, chunks)
    def _(chunk):
        load(chunk).start()

    for copy in airs:
        copy.start()
    pl.semaphore_wait(barrier, count - 1)

    @pl.loop(0, chunks)
    def _(chunk):
        load(chunk).wait()
        level = chunk // SPLITS

        @pl.loop(0, blocks)
        def _(block):
            at = pl.multiple_of((lax.rem(chunk, SPLITS) * blocks + block) * LANES, LANES)
            lanes = pl.ds(at, LANES)
            for s in range(species):
                send_low[chunk, block, s * LOW : (s + 1) * LOW, :] = tracer[
                    s, level, rows - LOW : rows, lanes
                ]
                send_high[chunk, block, s * HIGH : (s + 1) * HIGH, :] = tracer[
                    s, level, 0:HIGH, lanes
                ]

        forward(chunk).start()
        backward(chunk).start()

    sums[...] = jnp.zeros_like(sums)
    for copy in airs:
        copy.wait()

    @pl.loop(0, chunks)
    def _(chunk):
        level = chunk // SPLITS

        @pl.loop(0, blocks)
        def _(block):
            at = pl.multiple_of((lax.rem(chunk, SPLITS) * blocks + block) * LANES, LANES)
            lanes = pl.ds(at, LANES)
            air = air_before[level, :, lanes]
            for s in range(species):
                mass = tracer[s, level, :, lanes] * air
                sums[0, s] += jnp.sum(mass.reshape(rows // SUB, SUB, LANES), axis=0)

    @pl.loop(0, chunks)
    def _(chunk):
        level = chunk // SPLITS
        forward(chunk).wait_recv()
        backward(chunk).wait_recv()

        @pl.loop(0, blocks)
        def _(block):
            at = pl.multiple_of((lax.rem(chunk, SPLITS) * blocks + block) * LANES, LANES)
            lanes = pl.ds(at, LANES)
            fraction = frac_ref[:, lanes]
            pick = lax.broadcasted_iota(jnp.int32, fraction.shape, 0) == level
            fraction = jnp.sum(jnp.where(pick, fraction, 0.0), axis=0, keepdims=True)
            weights = cubic_weights(fraction)
            weights = [jnp.broadcast_to(item, (span, LANES)) for item in weights]
            row = lax.broadcasted_iota(jnp.int32, (SUB, LANES), 0)
            picks = []
            for d in range(rows // SUB):
                local = row - offsets[level, d * SUB : (d + 1) * SUB, lanes] + OFFMAX
                picks.append((lax.bitwise_and(local, SUB - 1), lax.shift_right_logical(local, 3)))
            for s in range(species):
                padded[s, 0:LOW, :] = recv_low[chunk, block, s * LOW : (s + 1) * LOW, :]
                padded[s, LOW : LOW + rows, :] = tracer[s, level, :, lanes]
                padded[s, LOW + rows : LOW + rows + HIGH, :] = recv_high[
                    chunk, block, s * HIGH : (s + 1) * HIGH, :
                ]
                taps = [padded[s, tap : tap + span, :] for tap in range(4)]
                cubic = weights[0] * taps[0] + weights[1] * taps[1]
                cubic = cubic + weights[2] * taps[2] + weights[3] * taps[3]
                lower = jnp.minimum(taps[1], taps[2])
                upper = jnp.maximum(taps[1], taps[2])
                values = jnp.minimum(jnp.maximum(cubic, lower), upper)
                total = sums[1, s]
                for d in range(rows // SUB):
                    spot, which = picks[d]
                    result = None
                    for h in range(4):
                        source = values[(d + h) * SUB : (d + h + 1) * SUB]
                        got = jnp.take_along_axis(
                            source, spot, axis=0, mode="promise_in_bounds"
                        )
                        result = got if result is None else jnp.where(which == h, got, result)
                    limited[s, level, d * SUB : (d + 1) * SUB, lanes] = result
                    total = total + result * air_after[level, d * SUB : (d + 1) * SUB, lanes]
                sums[1, s] = total

        store(chunk).start()

    lane = lax.broadcasted_iota(jnp.int32, (1, LANES), 1)
    line = jnp.zeros((1, LANES), jnp.float32)
    for which in range(2):
        for s in range(species):
            value = jnp.sum(sums[which, s], keepdims=True)
            line = jnp.where(lane == which * species + s, value, line)
    mine[...] = line
    masses[me] = line

    def share(step):
        return pltpu.make_async_remote_copy(
            src_ref=mine,
            dst_ref=masses.at[me],
            send_sem=mass_send.at[step],
            recv_sem=mass_recv.at[me],
            device_id={"lon": lax.rem(me + step, count)},
            device_id_type=MESH,
        )

    def arrive(step):
        source = lax.rem(me + count - step, count)
        return pltpu.make_async_remote_copy(
            src_ref=mine,
            dst_ref=masses.at[source],
            send_sem=mass_send.at[step],
            recv_sem=mass_recv.at[source],
            device_id={"lon": source},
            device_id_type=MESH,
        )

    @pl.loop(1, count)
    def _(step):
        share(step).start()

    @pl.loop(0, chunks)
    def _(chunk):
        forward(chunk).wait_send()
        backward(chunk).wait_send()
        store(chunk).wait()

    @pl.loop(1, count)
    def _(step):
        arrive(step).wait_recv()

    total = masses[0]
    for j in range(1, count):
        total = total + masses[j]
    grow = jnp.zeros((1, LANES), jnp.float32)
    for s in range(species):
        grow = jnp.where(lane == s, growth_ref[s], grow)
    later = pltpu.roll(total, LANES - species, axis=1)
    later = jnp.where(lane < species, later, 1.0)
    factor_ref[...] = total * (1.0 + grow) / later

    @pl.loop(1, count)
    def _(step):
        share(step).wait_send()


def on_device(tracer, offsets, frac, air_before, air_after, growth):
    species, levels, rows, lats = tracer.shape
    count = lax.axis_size("lon")
    chunks = levels * SPLITS
    blocks = lats // LANES // SPLITS
    any_spec = pl.BlockSpec(memory_space=pl.ANY)
    vmem_spec = pl.BlockSpec(memory_space=pltpu.VMEM)
    f32 = jnp.float32
    limited, factor = pl.pallas_call(
        functools.partial(transport_kernel, count),
        out_shape=(
            jax.ShapeDtypeStruct(tracer.shape, f32),
            jax.ShapeDtypeStruct((1, LANES), f32),
        ),
        in_specs=[
            pl.BlockSpec(memory_space=pltpu.SMEM),
            any_spec,
            any_spec,
            vmem_spec,
            any_spec,
            any_spec,
        ],
        out_specs=(any_spec, vmem_spec),
        scratch_shapes=[
            pltpu.VMEM(tracer.shape, f32),
            pltpu.VMEM(tracer.shape, f32),
            pltpu.VMEM(offsets.shape, jnp.int32),
            pltpu.VMEM(offsets.shape, f32),
            pltpu.VMEM(offsets.shape, f32),
            pltpu.VMEM((chunks, blocks, species * LOW, LANES), f32),
            pltpu.VMEM((chunks, blocks, species * HIGH, LANES), f32),
            pltpu.VMEM((chunks, blocks, species * LOW, LANES), f32),
            pltpu.VMEM((chunks, blocks, species * HIGH, LANES), f32),
            pltpu.VMEM((species, rows + 4 * SUB, LANES), f32),
            pltpu.VMEM((2, species, SUB, LANES), f32),
            pltpu.VMEM((1, LANES), f32),
            pltpu.VMEM((count, 1, LANES), f32),
            pltpu.SemaphoreType.DMA((chunks,)),
            pltpu.SemaphoreType.DMA((3,)),
            pltpu.SemaphoreType.DMA((chunks,)),
            pltpu.SemaphoreType.DMA((2, chunks)),
            pltpu.SemaphoreType.DMA((2, chunks)),
            pltpu.SemaphoreType.DMA((count,)),
            pltpu.SemaphoreType.DMA((count,)),
        ],
        compiler_params=pltpu.CompilerParams(
            collective_id=0, has_side_effects=True, vmem_limit_bytes=40 * 1024 * 1024
        ),
        name="transport",
    )(growth, tracer, offsets, frac, air_before, air_after)
    return limited * factor[0, :species][:, None, None, None]


def solution(mesh):
    placed = (
        P("scen", None, "lon", None),
        P(None, "lon", None),
        P(),
        P(None, "lon", None),
        P(None, "lon", None),
        P("scen"),
    )
    return jax.shard_map(
        on_device,
        mesh=mesh,
        in_specs=placed,
        out_specs=P("scen", None, "lon", None),
        check_vma=False,
    )
```

time: 136 us -> 60.8 us (0.45)
  other arithmetic: 59.5 us -> 2.53 us
  Pallas kernels: 0 us -> 51.2 us
  blocking collectives: 47.8 us -> 0 us
  waiting for transfers between devices: 15.3 us -> 0 us
  starting transfers between devices: 5.78 us -> 0 us
    pallas_call x0 -> x1, Pallas kernels: none -> 51.2 us  [on_device(): pl.pallas_call(functools.partial(transport_kernel, count), out_shape=(jax...]
    reduce_sum x2 -> x0, other arithmetic: 51 us -> none  [the longest x1 49.5 us: on_device(): after_local = jnp.sum(limited * air_after[None], axis=(1, 2, 3))]
    psum x1 -> x0, blocking collectives: 47.8 us -> none  [on_device(): after_total = lax.psum(after_local, 'lon')]
    ppermute x2 -> x0, waiting for transfers between devices: 15.3 us -> none  [the longest x1 15.3 us: with_halo(): lax.ppermute(lax.slice_in_dim(block, block.shape[dim] - width, None, axis...]
    ppermute x2 -> x0, starting transfers between devices: 5.78 us -> none  [the longest x1 5.23 us: with_halo(): lax.ppermute(lax.slice_in_dim(block, 0, width, axis=dim), axis, backward)]
    unnamed x12, local copies, waits for them, and re-layouts: 2.16 us -> 6.68 us
    slice x1 -> x0, local copies, waits for them, and re-layouts: 2.98 us -> none  [with_halo(): lax.slice_in_dim(block, block.shape[dim] - width, None, axis=dim)]
    eq x1 -> x0, other arithmetic: 2.72 us -> none  [limited_values(): chosen = offsets == offset_value]
  transfers between devices with their start and end apart: 2 -> 0, of which waited for: 1 -> 0; matrix products, arithmetic and copies ran while one was open for 5% -> 0% of each run, Pallas kernels for 0% -> 0%
where the time goes in v1:
time: 60.8 us; the launch traced here: 60.4 us
  Pallas kernels  51.2 us (84%)
  local copies, waits for them, and re-layouts  6.68 us (11%)
  other arithmetic  2.53 us (4%)
    pallas_call x1, Pallas kernels, on_device(): pl.pallas_call(functools.partial(transport_kernel, count), out_shape=(jax...  51.2 us
    unnamed x12, local copies, waits for them, and re-layouts  6.68 us
    mul x1, other arithmetic, on_device(): return limited * factor[0, :species][:, None, None, None]  2.53 us

profile of v1, /device:TPU:0, one launch (start us, length us, event | category | flops | bytes accessed | tf_op | source)
XLA Modules:
  0.0 60.4 jit_solution(12772105550716562232)
XLA Ops:
  0.0 0.0 copy-start
  0.0 2.2 %copy-done = f32[8,4,32,1024]{3,2,1,0:T(8,128)S(1)} copy-done((f32[8,4,32,1024]{3,2,1,0:T(8,128)S(1)}, f32[8,4,32,1024]{3,2,1,0:T(8,128)}, u32[]{:S(2)}) %copy-start) | copy-done | bytes 4194328
  2.2 0.0 copy-start.1
  2.2 1.0 %copy-done.1 = s32[4,32,1024]{2,1,0:T(8,128)S(1)} copy-done((s32[4,32,1024]{2,1,0:T(8,128)S(1)}, s32[4,32,1024]{2,1,0:T(8,128)}, u32[]{:S(2)}) %copy-start.1) | copy-done | bytes 524312
  3.2 0.0 copy-start.2
  3.2 1.0 %copy-done.2 = f32[4,32,1024]{2,1,0:T(8,128)S(1)} copy-done((f32[4,32,1024]{2,1,0:T(8,128)S(1)}, f32[4,32,1024]{2,1,0:T(8,128)}, u32[]{:S(2)}) %copy-start.2) | copy-done | bytes 524312
  4.3 0.0 copy-start.3
  4.3 1.0 %copy-done.3 = f32[4,32,1024]{2,1,0:T(8,128)S(1)} copy-done((f32[4,32,1024]{2,1,0:T(8,128)S(1)}, f32[4,32,1024]{2,1,0:T(8,128)}, u32[]{:S(2)}) %copy-start.3) | copy-done | bytes 524312
  5.3 0.0 copy-start.4
  5.3 0.7 %copy-done.4 = f32[4,1024]{1,0:T(4,128)S(1)} copy-done((f32[4,1024]{1,0:T(4,128)S(1)}, f32[4,1024]{1,0:T(4,128)}, u32[]{:S(2)}) %copy-start.4) | copy-done | bytes 16408
  6.0 0.0 copy-start.5
  6.0 0.7 %copy-done.5 = f32[8]{0:T(128)S(1)} copy-done((f32[8]{0:T(128)S(1)}, f32[8]{0:T(128)}, u32[]{:S(2)}) %copy-start.5) | copy-done | bytes 56
  6.7 51.2 %transport.1 = (f32[8,4,32,1024]{3,2,1,0:T(8,128)S(1)}, f32[1,128]{1,0:T(1,128)S(1)}) custom-call(f32[8]{0:T(128)S(1)} %copy-done.5, f32[8,4,32,1024]{3,2,1,0:T(8,128)S(1)} %copy-done, s32[4,32,1024]{2,1,0:T(8,128)S(1)} %copy-done.1, f32[4,1024]{1,0:T(4,128)S(1)} %copy-done.4, f32[4,32,1024]{2,1,0:T(8,128)S(1)} %copy-done.2, f32[4,32,1024]{2,1,0:T(8,128)S(1)} %copy-done.3), custom_call_target="tpu_custom_call" | custom-call | tf_op jit(solution)/shard_map/transport/pallas_call | solution.py:274
  57.9 2.5 %broadcast_multiply_fusion = f32[8,4,32,1024]{3,2,1,0:T(8,128)} fusion(f32[8,4,32,1024]{3,2,1,0:T(8,128)S(1)} %get-tuple-element.7, f32[8]{0:T(128)S(1)} %slice_bitcast_fusion), kind=kLoop, calls=%fused_computation | loop fusion | flops 1048576 | bytes 8388640 | tf_op jit(solution)/shard_map/mul | solution.py:316
  (1 shorter events, 0.0 us)
Async XLA Ops:
  0.0 2.2 %copy-start = (f32[8,4,32,1024]{3,2,1,0:T(8,128)S(1)}, f32[8,4,32,1024]{3,2,1,0:T(8,128)}, u32[]{:S(2)}) copy-start(f32[8,4,32,1024]{3,2,1,0:T(8,128)} %tracer_hbm.1) | copy-start | bytes 12582916
  2.2 1.0 %copy-start.1 = (s32[4,32,1024]{2,1,0:T(8,128)S(1)}, s32[4,32,1024]{2,1,0:T(8,128)}, u32[]{:S(2)}) copy-start(s32[4,32,1024]{2,1,0:T(8,128)} %offsets_hbm.1) | copy-start | bytes 1572868
  3.2 1.0 %copy-start.2 = (f32[4,32,1024]{2,1,0:T(8,128)S(1)}, f32[4,32,1024]{2,1,0:T(8,128)}, u32[]{:S(2)}) copy-start(f32[4,32,1024]{2,1,0:T(8,128)} %before_hbm.1) | copy-start | bytes 1572868
  4.3 1.0 %copy-start.3 = (f32[4,32,1024]{2,1,0:T(8,128)S(1)}, f32[4,32,1024]{2,1,0:T(8,128)}, u32[]{:S(2)}) copy-start(f32[4,32,1024]{2,1,0:T(8,128)} %after_hbm.1) | copy-start | bytes 1572868
  5.3 0.7 %copy-start.4 = (f32[4,1024]{1,0:T(4,128)S(1)}, f32[4,1024]{1,0:T(4,128)}, u32[]{:S(2)}) copy-start(f32[4,1024]{1,0:T(4,128)} %frac_ref.1) | copy-start | bytes 49156
  6.0 0.7 %copy-start.5 = (f32[8]{0:T(128)S(1)}, f32[8]{0:T(128)}, u32[]{:S(2)}) copy-start(f32[8]{0:T(128)} %growth_ref.1) | copy-start | bytes 100

commit v2 on v1

--- a/solution.py
+++ b/solution.py
@@ -12,7 +12,7 @@
 HIGH = OFFMAX + 2
 LANES = 128
 SUB = 8
-SPLITS = 2
+SPLITS = 4
 MESH = pl.DeviceIdType.MESH
 
 
@@ -26,12 +26,12 @@
 
 def transport_kernel(
     count,
-    growth_ref,
     tracer_hbm,
     offsets_hbm,
-    frac_ref,
+    frac_hbm,
     before_hbm,
     after_hbm,
+    growth_hbm,
     limited_hbm,
     factor_ref,
     tracer,
@@ -39,6 +39,8 @@
     offsets,
     air_before,
     air_after,
+    frac_ref,
+    growth_ref,
     send_low,
     send_high,
     recv_low,
@@ -82,6 +84,8 @@
         pltpu.make_async_copy(before_hbm, air_before, air_sem.at[0]),
         pltpu.make_async_copy(offsets_hbm, offsets, air_sem.at[1]),
         pltpu.make_async_copy(after_hbm, air_after, air_sem.at[2]),
+        pltpu.make_async_copy(frac_hbm, frac_ref, air_sem.at[3]),
+        pltpu.make_async_copy(growth_hbm, growth_ref, air_sem.at[4]),
     ]
 
     def forward(chunk):
@@ -104,23 +108,7 @@
             device_id_type=MESH,
         )
 
-    barrier = pltpu.get_barrier_semaphore()
-
-    @pl.loop(1, count)
-    def _(step):
-        peer = lax.rem(me + step, count)
-        pl.semaphore_signal(barrier, inc=1, device_id={"lon": peer}, device_id_type=MESH)
-
-    @pl.loop(0, chunks)
-    def _(chunk):
-        load(chunk).start()
-
-    for copy in airs:
-        copy.start()
-    pl.semaphore_wait(barrier, count - 1)
-
-    @pl.loop(0, chunks)
-    def _(chunk):
+    def pack(chunk):
         load(chunk).wait()
         level = chunk // SPLITS
 
@@ -136,6 +124,28 @@
                     s, level, 0:HIGH, lanes
                 ]
 
+    load(0).start()
+    barrier = pltpu.get_barrier_semaphore()
+
+    @pl.loop(1, count)
+    def _(step):
+        peer = lax.rem(me + step, count)
+        pl.semaphore_signal(barrier, inc=1, device_id={"lon": peer}, device_id_type=MESH)
+
+    @pl.loop(1, chunks)
+    def _(chunk):
+        load(chunk).start()
+
+    for copy in airs:
+        copy.start()
+    pack(0)
+    pl.semaphore_wait(barrier, count - 1)
+    forward(0).start()
+    backward(0).start()
+
+    @pl.loop(1, chunks)
+    def _(chunk):
+        pack(chunk)
         forward(chunk).start()
         backward(chunk).start()
 
@@ -155,6 +165,16 @@
             for s in range(species):
                 mass = tracer[s, level, :, lanes] * air
                 sums[0, s] += jnp.sum(mass.reshape(rows // SUB, SUB, LANES), axis=0)
+
+    lane = lax.broadcasted_iota(jnp.int32, (1, LANES), 1)
+
+    def gathered(which, line):
+        for s in range(species):
+            value = jnp.sum(sums[which, s], keepdims=True)
+            line = jnp.where(lane == which * species + s, value, line)
+        return line
+
+    mine[...] = gathered(0, jnp.zeros((1, LANES), jnp.float32))
 
     @pl.loop(0, chunks)
     def _(chunk):
@@ -204,12 +224,7 @@
 
         store(chunk).start()
 
-    lane = lax.broadcasted_iota(jnp.int32, (1, LANES), 1)
-    line = jnp.zeros((1, LANES), jnp.float32)
-    for which in range(2):
-        for s in range(species):
-            value = jnp.sum(sums[which, s], keepdims=True)
-            line = jnp.where(lane == which * species + s, value, line)
+    line = gathered(1, mine[...])
     mine[...] = line
     masses[me] = line
 
@@ -269,6 +284,7 @@
     chunks = levels * SPLITS
     blocks = lats // LANES // SPLITS
     any_spec = pl.BlockSpec(memory_space=pl.ANY)
+    hbm_spec = pl.BlockSpec(memory_space=pltpu.HBM)
     vmem_spec = pl.BlockSpec(memory_space=pltpu.VMEM)
     f32 = jnp.float32
     limited, factor = pl.pallas_call(
@@ -277,14 +293,7 @@
             jax.ShapeDtypeStruct(tracer.shape, f32),
             jax.ShapeDtypeStruct((1, LANES), f32),
         ),
-        in_specs=[
-            pl.BlockSpec(memory_space=pltpu.SMEM),
-            any_spec,
-            any_spec,
-            vmem_spec,
-            any_spec,
-            any_spec,
-        ],
+        in_specs=[hbm_spec] * 6,
         out_specs=(any_spec, vmem_spec),
         scratch_shapes=[
             pltpu.VMEM(tracer.shape, f32),
@@ -292,6 +301,8 @@
             pltpu.VMEM(offsets.shape, jnp.int32),
             pltpu.VMEM(offsets.shape, f32),
             pltpu.VMEM(offsets.shape, f32),
+            pltpu.VMEM(frac.shape, f32),
+            pltpu.SMEM(growth.shape, f32),
             pltpu.VMEM((chunks, blocks, species * LOW, LANES), f32),
             pltpu.VMEM((chunks, blocks, species * HIGH, LANES), f32),
             pltpu.VMEM((chunks, blocks, species * LOW, LANES), f32),
@@ -301,7 +312,7 @@
             pltpu.VMEM((1, LANES), f32),
             pltpu.VMEM((count, 1, LANES), f32),
             pltpu.SemaphoreType.DMA((chunks,)),
-            pltpu.SemaphoreType.DMA((3,)),
+            pltpu.SemaphoreType.DMA((5,)),
             pltpu.SemaphoreType.DMA((chunks,)),
             pltpu.SemaphoreType.DMA((2, chunks)),
             pltpu.SemaphoreType.DMA((2, chunks)),
@@ -309,10 +320,10 @@
             pltpu.SemaphoreType.DMA((count,)),
         ],
         compiler_params=pltpu.CompilerParams(
-            collective_id=0, has_side_effects=True, vmem_limit_bytes=40 * 1024 * 1024
+            collective_id=0, has_side_effects=True, vmem_limit_bytes=58 * 1024 * 1024
         ),
         name="transport",
-    )(growth, tracer, offsets, frac, air_before, air_after)
+    )(tracer, offsets, frac, air_before, air_after, growth)
     return limited * factor[0, :species][:, None, None, None]
 
 

time: 60.8 us -> 57 us (0.938)
  local copies, waits for them, and re-layouts: 6.68 us -> 0.64 us
  other arithmetic: 2.53 us -> 5.1 us
    unnamed x12 -> x0, local copies, waits for them, and re-layouts: 6.68 us -> none
    mul x1, other arithmetic: 2.53 us -> 5.1 us  [on_device(): return limited * factor[0, :species][:, None, None, None]]
    mul x1, local copies, waits for them, and re-layouts: 0.01 us -> 0.64 us  [on_device(): return limited * factor[0, :species][:, None, None, None]]
where the time goes in v2:
time: 57 us; the launch traced here: 56.8 us
  Pallas kernels  51.1 us (90%)
  other arithmetic  5.1 us (9%)
  local copies, waits for them, and re-layouts  0.64 us (1%)
    pallas_call x1, Pallas kernels, on_device(): pl.pallas_call(functools.partial(transport_kernel, count), out_shape=(jax...  51.1 us
    mul x1, other arithmetic, on_device(): return limited * factor[0, :species][:, None, None, None]  5.1 us

profile of v2, /device:TPU:0, one launch (start us, length us, event | category | flops | bytes accessed | tf_op | source)
XLA Modules:
  0.0 56.8 jit_solution(17684047889748244289)
XLA Ops:
  0.0 51.1 %transport.1 = (f32[8,4,32,1024]{3,2,1,0:T(8,128)}, f32[1,128]{1,0:T(1,128)}) custom-call(f32[8,4,32,1024]{3,2,1,0:T(8,128)} %tracer_hbm.1, s32[4,32,1024]{2,1,0:T(8,128)} %offsets_hbm.1, f32[4,1024]{1,0:T(4,128)} %frac_hbm.1, f32[4,32,1024]{2,1,0:T(8,128)} %before_hbm.1, f32[4,32,1024]{2,1,0:T(8,128)} %after_hbm.1, f32[8]{0:T(128)} %growth_hbm.1), custom_call_target="tpu_custom_call" | custom-call | tf_op jit(solution)/shard_map/transport/pallas_call | solution.py:290
  51.1 0.6 %slice_bitcast_fusion = f32[8]{0:T(128)S(1)} fusion(f32[1,128]{1,0:T(1,128)} %get-tuple-element.8), kind=kLoop, calls=%fused_computation.1 | loop fusion | bytes 64 | tf_op jit(solution)/shard_map/mul | solution.py:327
  51.7 5.1 %broadcast_multiply_fusion = f32[8,4,32,1024]{3,2,1,0:T(8,128)} fusion(f32[8,4,32,1024]{3,2,1,0:T(8,128)} %get-tuple-element.7, f32[8]{0:T(128)S(1)} %slice_bitcast_fusion), kind=kLoop, calls=%fused_computation | loop fusion | flops 1048576 | bytes 8388640 | tf_op jit(solution)/shard_map/mul | solution.py:327

commit v3 on v2

--- a/solution.py
+++ b/solution.py
@@ -276,6 +276,45 @@
     @pl.loop(1, count)
     def _(step):
         share(step).wait_send()
+
+
+def scale_kernel(
+    limited_hbm, factor_hbm, scaled_hbm, values, factor, read_sem, write_sem, factor_sem
+):
+    species, levels = values.shape[:2]
+    ready = pltpu.make_async_copy(factor_hbm, factor, factor_sem)
+    ready.start()
+
+    def read(s, level):
+        return pltpu.make_async_copy(
+            limited_hbm.at[s, level], values.at[s, level], read_sem.at[s, level]
+        )
+
+    def write(s, level):
+        return pltpu.make_async_copy(
+            values.at[s, level], scaled_hbm.at[s, level], write_sem.at[s, level]
+        )
+
+    @pl.loop(0, species)
+    def _(s):
+        for level in range(levels):
+            read(s, level).start()
+
+    ready.wait()
+    lane = lax.broadcasted_iota(jnp.int32, (1, LANES), 1)
+
+    @pl.loop(0, species)
+    def _(s):
+        scale = jnp.sum(jnp.where(lane == s, factor[...], 0.0), axis=1, keepdims=True)
+        for level in range(levels):
+            read(s, level).wait()
+            values[s, level] = values[s, level] * scale
+            write(s, level).start()
+
+    @pl.loop(0, species)
+    def _(s):
+        for level in range(levels):
+            write(s, level).wait()
 
 
 def on_device(tracer, offsets, frac, air_before, air_after, growth):
@@ -324,7 +363,21 @@
         ),
         name="transport",
     )(tracer, offsets, frac, air_before, air_after, growth)
-    return limited * factor[0, :species][:, None, None, None]
+    return pl.pallas_call(
+        scale_kernel,
+        out_shape=jax.ShapeDtypeStruct(tracer.shape, f32),
+        in_specs=[any_spec, any_spec],
+        out_specs=any_spec,
+        scratch_shapes=[
+            pltpu.VMEM(tracer.shape, f32),
+            pltpu.VMEM((1, LANES), f32),
+            pltpu.SemaphoreType.DMA((species, levels)),
+            pltpu.SemaphoreType.DMA((species, levels)),
+            pltpu.SemaphoreType.DMA,
+        ],
+        compiler_params=pltpu.CompilerParams(vmem_limit_bytes=58 * 1024 * 1024),
+        name="scale",
+    )(limited, factor)
 
 
 def solution(mesh):

time: 57 us -> 55.7 us (0.977)
  other arithmetic: 5.1 us -> 0 us
  Pallas kernels: 51.1 us -> 55.5 us
  local copies, waits for them, and re-layouts: 0.64 us -> 0 us
    mul x1 -> x0, other arithmetic: 5.1 us -> none  [on_device(): return limited * factor[0, :species][:, None, None, None]]
    pallas_call x0 -> x1, Pallas kernels: none -> 4.48 us  [on_device(): pl.pallas_call(scale_kernel, out_shape=jax.ShapeDtypeStruct(tracer.shape,...]
    mul x1 -> x0, local copies, waits for them, and re-layouts: 0.64 us -> none  [on_device(): return limited * factor[0, :species][:, None, None, None]]
where the time goes in v3:
time: 55.7 us; the launch traced here: 55.5 us
  Pallas kernels  55.5 us (100%)
    pallas_call x1, Pallas kernels, on_device(): pl.pallas_call(functools.partial(transport_kernel, count), out_shape=(jax...  51.1 us
    pallas_call x1, Pallas kernels, on_device(): pl.pallas_call(scale_kernel, out_shape=jax.ShapeDtypeStruct(tracer.shape,...  4.48 us

profile of v3, /device:TPU:0, one launch (start us, length us, event | category | flops | bytes accessed | tf_op | source)
XLA Modules:
  0.0 55.5 jit_solution(17999130804693123295)
XLA Ops:
  0.0 51.1 %transport.1 = (f32[8,4,32,1024]{3,2,1,0:T(8,128)}, f32[1,128]{1,0:T(1,128)}) custom-call(f32[8,4,32,1024]{3,2,1,0:T(8,128)} %tracer_hbm.1, s32[4,32,1024]{2,1,0:T(8,128)} %offsets_hbm.1, f32[4,1024]{1,0:T(4,128)} %frac_hbm.1, f32[4,32,1024]{2,1,0:T(8,128)} %before_hbm.1, f32[4,32,1024]{2,1,0:T(8,128)} %after_hbm.1, f32[8]{0:T(128)} %growth_hbm.1), custom_call_target="tpu_custom_call" | custom-call | tf_op jit(solution)/shard_map/transport/pallas_call | solution.py:329
  51.1 4.5 %scale.1 = f32[8,4,32,1024]{3,2,1,0:T(8,128)} custom-call(f32[8,4,32,1024]{3,2,1,0:T(8,128)} %get-tuple-element.7.limited_hbm, f32[1,128]{1,0:T(1,128)} %get-tuple-element.8.factor_hbm), custom_call_target="tpu_custom_call" | custom-call | tf_op jit(solution)/shard_map/scale/pallas_call | solution.py:366
